TPU v7x, 32 devices: a whole 2x2x4 slice. The times are simulated.
32 devices in a mesh: seq: 16 (over z, x, core), tp: 2 (over y).
Axes of the slice: x: 2, y: 2, z: 4, core: 2. Of those that a mesh axis runs over, the one named last changes fastest.
Arguments:
- hidden_in: bfloat16 [2048, 4096], P('seq', 'tp'), may hold values from -64 to 64
- span_order: int32 [16], replicated, may hold values from 0 to 15, each once
- norm_gain: bfloat16 [4096], P('tp'), may hold values from 0.099609375 to 1.8984375
- w_query: bfloat16 [4096, 4096], P('seq', 'tp'), may hold values from -0.09375 to 0.09375
- bias_query: bfloat16 [4096], P('tp'), may hold values from -14 to 14
- key_value_weight: bfloat16 [4096, 2, 1024], P('seq', None, 'tp'), may hold values from -0.09375 to 0.09375
- bias_kv: bfloat16 [2, 1024], P(None, 'tp'), may hold values from -14 to 14
- w_out: bfloat16 [4096, 4096], P('tp', 'seq'), may hold values from -0.09375 to 0.09375
- post_gain: bfloat16 [4096], P('tp'), may hold values from 0.099609375 to 1.8984375
Outputs:
- attn_out: bfloat16 [2048, 4096], P('seq', 'tp')
- normed: bfloat16 [2048, 4096], P('seq', 'tp')
Inputs may be any that keep to these rules, and one draw needn't show every extreme that they name: Each span number appears once; row r of hidden_in belongs to span span_order[r // 128].
All inputs are finite; a program needn't handle non-finite values.
Results may differ from a plain program's by a relative error of at most 0.014.
Values may be sent and summed in bfloat16 or wider, within the bound.
A program may use at most 128 MiB of HBM per device.

v0:
```python
import math
import jax
import jax.numpy as jnp
from jax import lax
from jax.sharding import PartitionSpec as P

MODEL_WIDTH = 4096
HEAD_SIZE = 128
GROUP = 4
eps = 1e-06
rope_base = 1000000.0


def apply_rotary(field, token_positions):
    half = field.shape[-1] // 2
    inverse = jnp.exp(-math.log(rope_base) * jnp.arange(half, dtype=jnp.float32) / half)
    angles = token_positions.astype(jnp.float32)[:, None] * inverse[None, :]
    cosine = jnp.cos(angles)[:, None, :]
    sine = jnp.sin(angles)[:, None, :]
    first = field[..., :half]
    second = field[..., half:]
    return jnp.concatenate(
        [first * cosine - second * sine, second * cosine + first * sine], axis=-1
    )


def span_lookup(order, devices):
    table_ids = jnp.arange(order.shape[0], dtype=jnp.int32)
    return jnp.sum(jnp.where(devices[:, None] == table_ids[None, :], order[None, :], 0), axis=1)


def per_device(
    hidden_in,
    span_order,
    norm_gain,
    w_query,
    bias_query,
    key_value_weight,
    bias_kv,
    w_out,
    post_gain,
):
    tok_rows = hidden_in.shape[0]
    seq_index = lax.axis_index("seq")
    own_span = span_lookup(span_order, jnp.full((1,), seq_index, jnp.int32))[0]
    token_positions = own_span * tok_rows + jnp.arange(tok_rows, dtype=jnp.int32)
    local = hidden_in.astype(jnp.float32)
    raw_rows, gains = (
        lax.all_gather(hidden_in, "tp", axis=1, tiled=True),
        lax.all_gather(norm_gain[None, :], "tp", axis=1, tiled=True),
    )
    full_rows = raw_rows.astype(jnp.float32)
    meansq = jnp.mean(full_rows * full_rows, axis=1, keepdims=True)
    normed_in = (full_rows * lax.rsqrt(meansq + eps) * gains.astype(jnp.float32)).astype(
        jnp.bfloat16
    )
    columns = normed_in
    query_proj = jnp.dot(
        columns,
        lax.all_gather(w_query, "seq", axis=0, tiled=True),
        preferred_element_type=jnp.float32,
    )
    columns = normed_in
    pair_proj = jnp.einsum(
        "tr,rkc->tkc",
        columns,
        lax.all_gather(key_value_weight, "seq", axis=0, tiled=True),
        preferred_element_type=jnp.float32,
    )
    query_heads = w_query.shape[1] // HEAD_SIZE
    kv_heads = key_value_weight.shape[2] // HEAD_SIZE
    query_proj = query_proj + bias_query.astype(jnp.float32)[None, :]
    queries = apply_rotary(
        query_proj.reshape(tok_rows, query_heads, HEAD_SIZE), token_positions
    ).astype(jnp.bfloat16)
    pair_proj = pair_proj + bias_kv.astype(jnp.float32)[None, :, :]
    rotated_keys = apply_rotary(
        pair_proj[:, 0, :].reshape(tok_rows, kv_heads, HEAD_SIZE), token_positions
    )
    rotated_keys = rotated_keys.astype(jnp.bfloat16).reshape(tok_rows, kv_heads * HEAD_SIZE)
    value_rows = pair_proj[:, 1, :].astype(jnp.bfloat16)
    grouped = (
        queries.reshape(tok_rows, kv_heads, GROUP, HEAD_SIZE)
        .transpose(1, 2, 0, 3)
        .reshape(kv_heads, GROUP * tok_rows, HEAD_SIZE)
    )
    query_pos = jnp.tile(token_positions, GROUP)
    last_query = jnp.max(token_positions)
    scale = 1.0 / math.sqrt(HEAD_SIZE)
    start_state = (
        jnp.full((kv_heads, GROUP * tok_rows), -1e30, jnp.float32),
        jnp.zeros((kv_heads, GROUP * tok_rows), jnp.float32),
        jnp.zeros((kv_heads, GROUP * tok_rows, HEAD_SIZE), jnp.float32),
    )
    key_piece = lax.all_gather(rotated_keys, "seq", axis=0, tiled=True)
    value_piece = lax.all_gather(value_rows, "seq", axis=0, tiled=True)
    count = key_piece.shape[0]
    block = math.gcd(count, 1536)

    def visit(step, state):
        first = step * block
        key_block = lax.dynamic_slice_in_dim(key_piece, first, block, 0).reshape(
            block, kv_heads, HEAD_SIZE
        )
        value_block = lax.dynamic_slice_in_dim(value_piece, first, block, 0).reshape(
            block, kv_heads, HEAD_SIZE
        )
        row_ids = first + jnp.arange(block, dtype=jnp.int32)
        key_pos = span_lookup(span_order, row_ids // tok_rows) * tok_rows + row_ids % tok_rows

        def update(current):
            maxima, totals, sums = current
            scores = (
                jnp.einsum("kqd,nkd->kqn", grouped, key_block, preferred_element_type=jnp.float32)
                * scale
            )
            allowed = (key_pos[None, :] <= query_pos[:, None])[None, :, :]
            scores = jnp.where(allowed, scores, -1e30)
            fresh = jnp.maximum(maxima, jnp.max(scores, axis=2))
            weights = jnp.where(allowed, jnp.exp(scores - fresh[:, :, None]), 0.0)
            factor = jnp.exp(maxima - fresh)
            totals = totals * factor + jnp.sum(weights, axis=2)
            sums = sums * factor[:, :, None] + jnp.einsum(
                "kqn,nkd->kqd",
                weights.astype(jnp.bfloat16),
                value_block,
                preferred_element_type=jnp.float32,
            )
            return (fresh, totals, sums)

        return lax.cond(jnp.min(key_pos) <= last_query, update, lambda current: current, state)

    maxima, totals, sums = lax.fori_loop(0, count // block, visit, start_state)
    attended = (sums / totals[:, :, None]).astype(jnp.bfloat16)
    attended = (
        attended.reshape(kv_heads, GROUP, tok_rows, HEAD_SIZE)
        .transpose(2, 0, 1, 3)
        .reshape(tok_rows, query_heads * HEAD_SIZE)
    )
    partial_out = jnp.dot(
        attended,
        lax.all_gather(w_out, "seq", axis=1, tiled=True),
        preferred_element_type=jnp.float32,
    )
    mixed = lax.psum_scatter(
        partial_out.astype(jnp.bfloat16), "tp", scatter_dimension=1, tiled=True
    ).astype(jnp.float32)
    attn_out = mixed.astype(jnp.bfloat16)
    stream = local + mixed
    post_sq = lax.psum(jnp.sum(stream * stream, axis=1), "tp")
    normed = (
        stream
        * lax.rsqrt(post_sq / MODEL_WIDTH + eps)[:, None]
        * post_gain.astype(jnp.float32)[None, :]
    ).astype(jnp.bfloat16)
    return (attn_out, normed)


def solution(mesh):
    placed = (
        P("seq", "tp"),
        P(),
        P("tp"),
        P("seq", "tp"),
        P("tp"),
        P("seq", None, "tp"),
        P(None, "tp"),
        P("tp", "seq"),
        P("tp"),
    )
    return jax.shard_map(
        per_device,
        mesh=mesh,
        in_specs=placed,
        out_specs=(P("seq", "tp"), P("seq", "tp")),
        check_vma=False,
    )
```

profile of v0, /device:TPU:0, one launch (start us, length us, event | category | flops | bytes accessed | tf_op | source)
XLA Modules:
  0.0 499.7 jit_solution(17849845767442077635)
XLA Ops:
  7.2 0.7 all-gather.9.cloned.1.call-update
  7.9 1.9 copy.44
  9.9 5.5 %all-gather = bf16[4096]{0:T(1024)(128)(2,1)S(1)} all-gather(bf16[2048]{0:T(1024)(128)(2,1)} %param.15), channel_id=2, replica_groups=mesh['seq'=16,'tp'=2] {'tp'}, dimensions={0}, use_global_device_ids=true | all-gather | bytes 12288 | tf_op jit(solution)/shard_map/all_gather | solution.py:50
  15.4 0.7 convert_element_type.69
  16.1 17.4 %all-gather.9.cloned.1.call-done = bf16[128,4096]{1,0:T(8,128)(2,1)} async-done(((bf16[128,2048]{1,0:T(8,128)(2,1)}), bf16[128,4096]{1,0:T(8,128)(2,1)}) %all-gather.9.cloned.1.call-update) | async-done | bytes 1048592 | tf_op jit(solution)/shard_map/all_gather | solution.py:49
  33.6 1.5 fusion.18
  35.1 75.6 %all-gather.11.cloned.1.call-done = bf16[4096,2,512]{2,0,1:T(8,128)(2,1)} async-done(((bf16[256,2,512]{2,0,1:T(8,128)(2,1)}), bf16[4096,2,512]{2,0,1:T(8,128)(2,1)}) %all-gather.11.cloned.1.call-update) | async-done | bytes 8388624 | tf_op jit(solution)/shard_map/all_gather | solution.py:67
  110.7 5.0 %convolution_add_fusion.1 = f32[128,2,512]{2,0,1:T(8,128)S(1)} fusion(bf16[4096,2,512]{2,0,1:T(8,128)(2,1)} %all-gather.11.cloned.1.call-done, bf16[128,4096]{1,0:T(8,128)(2,1)} %all-gather.9.cloned.1.call-done, f32[4096]{0:T(1024)S(1)} %mul.210, f32[128]{0:T(128)S(1)} %add_rsqrt_fusion.1, f32[2,512]{1,0:T(2,128)S(1)} %convert_element_type.69), kind=kOutput, calls=%fused_computation.39 | convolution fusion | flops 1075970048 | bytes 9982464 | tf_op jit(solution)/shard_map/tr,rkc->tkc/dot_general | solution.py:64
  115.7 0.7 slice.40
  119.3 0.8 copy.45
  121.5 35.1 %all-gather.19.cloned.1.call-done = bf16[2048,1,512]{2,0,1:T(8,128)(2,1)} async-done(((bf16[128,1,512]{2,0,1:T(8,128)(2,1)}), bf16[2048,1,512]{2,0,1:T(8,128)(2,1)}) %all-gather.19.cloned.1.call-update) | async-done | bytes 2097168 | tf_op jit(solution)/shard_map/all_gather | solution.py:96
  156.6 2.9 copy.48
  159.5 124.3 %all-gather.15.cloned.1.call-done = bf16[4096,2048]{1,0:T(8,128)(2,1)} async-done(((bf16[256,2048]{1,0:T(8,128)(2,1)}), bf16[4096,2048]{1,0:T(8,128)(2,1)}) %all-gather.15.cloned.1.call-update) | async-done | bytes 16777232 | tf_op jit(solution)/shard_map/all_gather | solution.py:60
  283.8 8.2 %fusion.21 = f32[16,8,16,128]{3,1,2,0:T(8,128)S(1)} fusion(bf16[4096,2048]{1,0:T(8,128)(2,1)} %all-gather.15.cloned.1.call-done, f32[2048]{0:T(1024)S(1)} %convert_element_type.72, bf16[128,4096]{1,0:T(8,128)(2,1)S(1)} %copy-done, f32[4096]{0:T(1024)S(1)} %mul.210, f32[128]{0:T(128)S(1)} %add_rsqrt_fusion.1), kind=kOutput, calls=%fused_computation.38 | convolution fusion | flops 2149842944 | bytes 18899456 | tf_op jit(solution)/shard_map/dot_general | solution.py:58
  293.3 32.3 %all-gather.13.cloned.1.call-done = bf16[2048,512]{0,1:T(8,128)(2,1)} async-done(((bf16[128,512]{0,1:T(8,128)(2,1)}), bf16[2048,512]{0,1:T(8,128)(2,1)}) %all-gather.13.cloned.1.call-update) | async-done | bytes 2097168 | tf_op jit(solution)/shard_map/all_gather | solution.py:95
  325.6 1.1 broadcast_in_dim.105
  326.7 33.3 %while.20 = (s32[]{:T(128)}, f32[4,512]{1,0:T(4,128)S(1)}, f32[4,512]{1,0:T(4,128)S(1)}, f32[4,512,128]{2,1,0:T(8,128)}, s32[16]{0:T(128)S(1)}, /*index=5*/s32[]...) while((s32[]{:T(128)}, f32[4,512]{1,0:T(4,128)S(1)}, ...), condition=%wide.region_10.11_spmd.clone, body=%wide.region_3.10_spmd.clone.sunk | while | flops 551332864 | bytes 27935672 | solution.py:133
  328.7 6.3 %conditional.3 = ((f32[4,512]{1,0:T(4,128)S(1)}, f32[4,512]{1,0:T(4,128)S(1)}, f32[4,512,128]{2,1,0:T(8,128)})) conditional(s32[]{:T(128)} %convert_element_type.117, (f32[4,512]{1,0:T(4,128)S(1)}, f32[4,512]{1,0:T(4,128)S(1)}, f32[4,512,128]{2,1,0:T(8,128)}) %tuple.77, (s32[512]{0:T(512)S(1)}, s32[128]{0:T(128)S(1)}, s32[]{:T(128)}, ...), branch_computations={%region_6.6_spmd, %region_7.9_spmd} | conditional | flops 551292928 | bytes 27925118 | solution.py:131
  328.7 1.1 constant_dynamic-slice_fusion
  330.1 1.0 fusion.2
  331.2 1.0 fusion.4
  332.2 1.8 fusion.8
  334.0 1.0 copy-done.3
  337.0 6.3 %conditional.3 = ((f32[4,512]{1,0:T(4,128)S(1)}, f32[4,512]{1,0:T(4,128)S(1)}, f32[4,512,128]{2,1,0:T(8,128)})) conditional(s32[]{:T(128)} %convert_element_type.117, (f32[4,512]{1,0:T(4,128)S(1)}, f32[4,512]{1,0:T(4,128)S(1)}, f32[4,512,128]{2,1,0:T(8,128)}) %tuple.77, (s32[512]{0:T(512)S(1)}, s32[128]{0:T(128)S(1)}, s32[]{:T(128)}, ...), branch_computations={%region_6.6_spmd, %region_7.9_spmd} | conditional | flops 551292928 | bytes 27925118 | solution.py:131
  337.0 1.2 constant_dynamic-slice_fusion
  338.5 1.0 fusion.2
  339.5 1.0 fusion.4
  340.6 1.8 fusion.8
  342.4 1.0 copy-done.3
  345.4 6.3 %conditional.3 = ((f32[4,512]{1,0:T(4,128)S(1)}, f32[4,512]{1,0:T(4,128)S(1)}, f32[4,512,128]{2,1,0:T(8,128)})) conditional(s32[]{:T(128)} %convert_element_type.117, (f32[4,512]{1,0:T(4,128)S(1)}, f32[4,512]{1,0:T(4,128)S(1)}, f32[4,512,128]{2,1,0:T(8,128)}) %tuple.77, (s32[512]{0:T(512)S(1)}, s32[128]{0:T(128)S(1)}, s32[]{:T(128)}, ...), branch_computations={%region_6.6_spmd, %region_7.9_spmd} | conditional | flops 551292928 | bytes 27925118 | solution.py:131
  345.4 1.1 constant_dynamic-slice_fusion
  346.8 1.0 fusion.2
  347.8 1.0 fusion.4
  348.9 1.8 fusion.8
  350.7 1.0 copy-done.3
  353.7 6.3 %conditional.3 = ((f32[4,512]{1,0:T(4,128)S(1)}, f32[4,512]{1,0:T(4,128)S(1)}, f32[4,512,128]{2,1,0:T(8,128)})) conditional(s32[]{:T(128)} %convert_element_type.117, (f32[4,512]{1,0:T(4,128)S(1)}, f32[4,512]{1,0:T(4,128)S(1)}, f32[4,512,128]{2,1,0:T(8,128)}) %tuple.77, (s32[512]{0:T(512)S(1)}, s32[128]{0:T(128)S(1)}, s32[]{:T(128)}, ...), branch_computations={%region_6.6_spmd, %region_7.9_spmd} | conditional | flops 551292928 | bytes 27925118 | solution.py:131
  353.7 1.1 constant_dynamic-slice_fusion
  355.1 1.0 fusion.2
  356.1 1.0 fusion.4
  357.2 1.8 fusion.8
  359.0 1.0 copy-done.3
  360.0 1.6 divide_convert_fusion
  361.8 94.8 %all-gather.17.cloned.1.call-done = bf16[2048,4096]{1,0:T(8,128)(2,1)} async-done(((bf16[2048,256]{1,0:T(8,128)(2,1)}), bf16[2048,4096]{1,0:T(8,128)(2,1)}) %all-gather.17.cloned.1.call-update) | async-done | bytes 16777232 | tf_op jit(solution)/shard_map/all_gather | solution.py:142
  456.6 9.2 %convolution_convert_fusion = bf16[128,4096]{1,0:T(8,128)(2,1)} fusion(bf16[128,2048]{0,1:T(8,128)(2,1)S(1)} %bitcast.47, bf16[2048,4096]{1,0:T(8,128)(2,1)} %all-gather.17.cloned.1.call-done), kind=kOutput, calls=%fused_computation.31 | convolution fusion | flops 2148007936 | bytes 18350080 | tf_op jit(solution)/shard_map/dot_general | solution.py:140
  465.9 18.7 %reduce-scatter.2.cloned.1.call-done = bf16[128,2048]{1,0:T(8,128)(2,1)} async-done(((bf16[128,4096]{1,0:T(8,128)(2,1)}), bf16[128,2048]{1,0:T(8,128)(2,1)}) %reduce-scatter.2.cloned.1.call-update) | async-done | bytes 524304 | tf_op jit(solution)/shard_map/reduce_scatter | solution.py:145
  484.6 1.3 multiply_reduce_fusion
  485.9 4.9 psum.7
  490.8 2.0 multiply_convert_fusion
  (89 shorter events, 9.4 us)
Async XLA Ops:
  7.2 26.4 %all-gather.9.cloned.1.call-start = ((), (), s32[]{:S(2)}) async-start(), calls=%async_computation.1 | async-start | bytes 1572864 | tf_op jit(solution)/shard_map/all_gather | solution.py:49
  7.9 102.8 %all-gather.11.cloned.1.call-start = ((), (), s32[]{:S(2)}) async-start(), calls=%async_computation.2 | async-start | bytes 8912896 | tf_op jit(solution)/shard_map/all_gather | solution.py:67
  9.9 146.8 %all-gather.19.cloned.1.call-start = ((), (), s32[]{:S(2)}) async-start(), calls=%async_computation.7 | async-start | bytes 2228224 | tf_op jit(solution)/shard_map/all_gather | solution.py:96
  35.1 81.9 %copy-start.4 = (s32[16]{0:T(128)S(1)}, s32[16]{0:T(128)}, u32[]{:S(2)}) copy-start(s32[16]{0:T(128)} %param.14) | copy-start | bytes 196
  115.7 5.2 %copy-start.5 = (bf16[2048]{0:T(1024)(128)(2,1)S(1)}, bf16[2048]{0:T(1024)(128)(2,1)}, u32[]{:S(2)}) copy-start(bf16[2048]{0:T(1024)(128)(2,1)} %param.17) | copy-start | bytes 12292
  116.4 167.4 %all-gather.15.cloned.1.call-start = ((), (), s32[]{:S(2)}) async-start(), calls=%async_computation.4 | async-start | bytes 17825792 | tf_op jit(solution)/shard_map/all_gather | solution.py:60
  117.0 166.8 %copy-start = (bf16[128,4096]{1,0:T(8,128)(2,1)S(1)}, bf16[128,4096]{1,0:T(8,128)(2,1)}, u32[]{:S(2)}) copy-start(bf16[128,4096]{1,0:T(8,128)(2,1)} %all-gather.9.cloned.1.call-done) | copy-start | bytes 3145732
  117.0 208.7 %all-gather.13.cloned.1.call-start = ((), (), s32[]{:S(2)}) async-start(), calls=%async_computation.3 | async-start | bytes 2228224 | tf_op jit(solution)/shard_map/all_gather | solution.py:95
  120.1 336.6 %all-gather.17.cloned.1.call-start = ((), (), s32[]{:S(2)}) async-start(), calls=%async_computation.5 | async-start | bytes 17825792 | tf_op jit(solution)/shard_map/all_gather | solution.py:142
  120.7 363.9 %reduce-scatter.2.cloned.1.call-start = ((), (), s32[]{:S(2)}) async-start(), calls=%async_computation.6 | async-start | bytes 1572864 | tf_op jit(solution)/shard_map/reduce_scatter | solution.py:145
  330.1 2.1 copy-start.2
  334.0 1.0 copy-start.3
  338.4 2.1 copy-start.2
  342.4 1.0 copy-start.3
  346.8 2.1 copy-start.2
  350.7 1.0 copy-start.3
  355.1 2.1 copy-start.2
  359.0 1.0 copy-start.3
  456.6 9.2 %copy-start.6 = (bf16[2048]{0:T(1024)(128)(2,1)S(1)}, bf16[2048]{0:T(1024)(128)(2,1)}, u32[]{:S(2)}) copy-start(bf16[2048]{0:T(1024)(128)(2,1)} %param.21) | copy-start | bytes 12292
  456.6 27.9 %copy-start.1 = (bf16[128,2048]{1,0:T(8,128)(2,1)S(1)}, bf16[128,2048]{1,0:T(8,128)(2,1)}, u32[]{:S(2)}) copy-start(bf16[128,2048]{1,0:T(8,128)(2,1)} %param.13) | copy-start | bytes 1572868
Sparse Core Ops, SparseCore 0:
  9.5 23.9 all-gather.8
  36.3 74.2 all-gather.10
  116.5 40.0 all-gather.18
  158.6 125.1 all-gather.14
  286.4 39.2 all-gather.12
  327.7 128.9 all-gather.16
  466.0 18.5 reduce-scatter.1
where the time goes:
time: 500 us
  waiting for transfers between devices  400 us (80%)
  matrix products  33.6 us (7%)
  other arithmetic  18.1 us (4%)
  local copies, waits for them, and re-layouts  16.7 us (3%)
  between operations  15 us (3%)
  blocking collectives  10.4 us (2%)
  loops' own time  5.46 us (1%)
    all_gather x1, waiting for transfers between devices, per_device(): lax.all_gather(w_query, 'seq', axis=0, tiled=True)  124 us
    all_gather x1, waiting for transfers between devices, per_device(): lax.all_gather(w_out, 'seq', axis=1, tiled=True)  94.8 us
    all_gather x1, waiting for transfers between devices, per_device(): lax.all_gather(key_value_weight, 'seq', axis=0, tiled=True)  75.6 us
    all_gather x1, waiting for transfers between devices, per_device(): value_piece = lax.all_gather(value_rows, 'seq', axis=0, tiled=True)  35.1 us
    all_gather x1, waiting for transfers between devices, per_device(): key_piece = lax.all_gather(rotated_keys, 'seq', axis=0, tiled=True)  32.3 us
    reduce_scatter x1, waiting for transfers between devices, per_device(): lax.psum_scatter(partial_out.astype(jnp.bfloat16), 'tp', scatter_dimensio...  18.7 us
    all_gather x1, waiting for transfers between devices, per_device(): lax.all_gather(hidden_in, 'tp', axis=1, tiled=True)  17.4 us
  transfers between devices with their start and end apart: 7, of which 7 were waited for; matrix products, arithmetic and copies ran while one was open for 9% of the time, Pallas kernels for 0%

commit v1 on v0

--- a/solution.py
+++ b/solution.py
@@ -93,7 +93,12 @@
         jnp.zeros((kv_heads, GROUP * tok_rows, HEAD_SIZE), jnp.float32),
     )
     key_piece = lax.all_gather(rotated_keys, "seq", axis=0, tiled=True)
-    value_piece = lax.all_gather(value_rows, "seq", axis=0, tiled=True)
+    ring = [value_rows]
+    for hop in range(15):
+        ring.append(lax.ppermute(ring[-1], "seq", [(dev, (dev + 1) % 16) for dev in range(16)]))
+    value_piece = jnp.roll(
+        jnp.concatenate(ring[::-1], axis=0), (lax.axis_index("seq") + 1) * ring[0].shape[0], axis=0
+    )
     count = key_piece.shape[0]
     block = math.gcd(count, 1536)
 

time: 500 us -> 470 us (0.940)
  waiting for transfers between devices: 400 us -> 367 us
    ppermute x0 -> x15, waiting for transfers between devices: none -> 140 us  [per_device(): lax.ppermute(ring[-1], 'seq', [(dev, (dev + 1) % 16) for dev in range(16)])]
    all_gather x1, waiting for transfers between devices: 124 us -> 0.02 us  [per_device(): lax.all_gather(w_query, 'seq', axis=0, tiled=True)]
    all_gather x1 -> x0, waiting for transfers between devices: 35.1 us -> none  [per_device(): value_piece = lax.all_gather(value_rows, 'seq', axis=0, tiled=True)]
    all_gather x1, waiting for transfers between devices: 32.3 us -> 21.7 us  [per_device(): key_piece = lax.all_gather(rotated_keys, 'seq', axis=0, tiled=True)]
  transfers between devices with their start and end apart: 7 -> 21, of which waited for: 7 -> 20; matrix products, arithmetic and copies ran while one was open for 9% -> 12% of each run, Pallas kernels for 0% -> 0%
where the time goes in v1:
time: 470 us; the launch traced here: 469 us
  waiting for transfers between devices  367 us (78%)
  matrix products  33.6 us (7%)
  other arithmetic  18.9 us (4%)
  local copies, waits for them, and re-layouts  18.1 us (4%)
  between operations  15.2 us (3%)
  blocking collectives  10.4 us (2%)
  loops' own time  5.45 us (1%)
    ppermute x15, waiting for transfers between devices, per_device(): lax.ppermute(ring[-1], 'seq', [(dev, (dev + 1) % 16) for dev in range(16)])  140 us
    all_gather x1, waiting for transfers between devices, per_device(): lax.all_gather(w_out, 'seq', axis=1, tiled=True)  94.7 us
    all_gather x1, waiting for transfers between devices, per_device(): lax.all_gather(key_value_weight, 'seq', axis=0, tiled=True)  75.6 us
    all_gather x1, waiting for transfers between devices, per_device(): key_piece = lax.all_gather(rotated_keys, 'seq', axis=0, tiled=True)  21.7 us
    reduce_scatter x1, waiting for transfers between devices, per_device(): lax.psum_scatter(partial_out.astype(jnp.bfloat16), 'tp', scatter_dimensio...  18.7 us
    all_gather x1, waiting for transfers between devices, per_device(): lax.all_gather(hidden_in, 'tp', axis=1, tiled=True)  14.4 us
  transfers between devices with their start and end apart: 21, of which 20 were waited for; matrix products, arithmetic and copies ran while one was open for 12% of the time, Pallas kernels for 0%

profile of v1, /device:TPU:0, one launch (start us, length us, event | category | flops | bytes accessed | tf_op | source)
XLA Modules:
  0.0 469.2 jit_solution(11110986045244681769)
XLA Ops:
  7.9 1.9 copy.44
  10.6 5.5 %all-gather = bf16[4096]{0:T(1024)(128)(2,1)S(1)} all-gather(bf16[2048]{0:T(1024)(128)(2,1)} %param.15), channel_id=2, replica_groups=mesh['seq'=16,'tp'=2] {'tp'}, dimensions={0}, use_global_device_ids=true | all-gather | bytes 12288 | tf_op jit(solution)/shard_map/all_gather | solution.py:50
  16.9 1.3 fusion.26
  19.1 14.4 %all-gather.7.cloned.1.call-done = bf16[128,4096]{1,0:T(8,128)(2,1)} async-done(((bf16[128,2048]{1,0:T(8,128)(2,1)}), bf16[128,4096]{1,0:T(8,128)(2,1)}) %all-gather.7.cloned.1.call-update) | async-done | bytes 1048592 | tf_op jit(solution)/shard_map/all_gather | solution.py:49
  33.6 1.5 fusion.18
  35.1 75.6 %all-gather.9.cloned.1.call-done = bf16[4096,2,512]{2,0,1:T(8,128)(2,1)} async-done(((bf16[256,2,512]{2,0,1:T(8,128)(2,1)}), bf16[4096,2,512]{2,0,1:T(8,128)(2,1)}) %all-gather.9.cloned.1.call-update) | async-done | bytes 8388624 | tf_op jit(solution)/shard_map/all_gather | solution.py:67
  110.7 5.0 %convolution_add_fusion.1 = f32[128,2,512]{2,0,1:T(8,128)S(1)} fusion(bf16[4096,2,512]{2,0,1:T(8,128)(2,1)} %all-gather.9.cloned.1.call-done, bf16[128,4096]{1,0:T(8,128)(2,1)} %all-gather.7.cloned.1.call-done, f32[4096]{0:T(1024)S(1)} %mul.214, f32[128]{0:T(128)S(1)} %add_rsqrt_fusion.1, f32[2,512]{1,0:T(2,128)S(1)} %convert_element_type.69), kind=kOutput, calls=%fused_computation.39 | convolution fusion | flops 1075970048 | bytes 9982464 | tf_op jit(solution)/shard_map/tr,rkc->tkc/dot_general | solution.py:64
  118.1 6.9 %collective-permute-done = bf16[128,512]{1,0:T(8,128)(2,1)S(1)} collective-permute-done((bf16[128,512]{1,0:T(8,128)(2,1)S(1)}, bf16[128,512]{1,0:T(8,128)(2,1)S(1)}, u32[]{:S(2)}, u32[]{:S(2)}) %collective-permute-start) | collective-permute-done | bytes 131104 | tf_op jit(solution)/shard_map/ppermute | solution.py:98
  125.0 10.0 %collective-permute-done.1 = bf16[128,512]{1,0:T(8,128)(2,1)S(1)} collective-permute-done((bf16[128,512]{1,0:T(8,128)(2,1)S(1)}, bf16[128,512]{1,0:T(8,128)(2,1)S(1)}, u32[]{:S(2)}, u32[]{:S(2)}) %collective-permute-start.1) | collective-permute-done | bytes 131104 | tf_op jit(solution)/shard_map/ppermute | solution.py:98
  135.0 10.0 %collective-permute-done.2 = bf16[128,512]{1,0:T(8,128)(2,1)S(1)} collective-permute-done((bf16[128,512]{1,0:T(8,128)(2,1)S(1)}, bf16[128,512]{1,0:T(8,128)(2,1)S(1)}, u32[]{:S(2)}, u32[]{:S(2)}) %collective-permute-start.2) | collective-permute-done | bytes 131104 | tf_op jit(solution)/shard_map/ppermute | solution.py:98
  145.0 10.0 %collective-permute-done.3 = bf16[128,512]{1,0:T(8,128)(2,1)S(1)} collective-permute-done((bf16[128,512]{1,0:T(8,128)(2,1)S(1)}, bf16[128,512]{1,0:T(8,128)(2,1)S(1)}, u32[]{:S(2)}, u32[]{:S(2)}) %collective-permute-start.3) | collective-permute-done | bytes 131104 | tf_op jit(solution)/shard_map/ppermute | solution.py:98
  155.1 9.9 %collective-permute-done.4 = bf16[128,512]{1,0:T(8,128)(2,1)S(1)} collective-permute-done((bf16[128,512]{1,0:T(8,128)(2,1)S(1)}, bf16[128,512]{1,0:T(8,128)(2,1)S(1)}, u32[]{:S(2)}, u32[]{:S(2)}) %collective-permute-start.4) | collective-permute-done | bytes 131104 | tf_op jit(solution)/shard_map/ppermute | solution.py:98
  165.0 7.2 %collective-permute-done.5 = bf16[128,512]{1,0:T(8,128)(2,1)S(1)} collective-permute-done((bf16[128,512]{1,0:T(8,128)(2,1)S(1)}, bf16[128,512]{1,0:T(8,128)(2,1)S(1)}, u32[]{:S(2)}, u32[]{:S(2)}) %collective-permute-start.5) | collective-permute-done | bytes 131104 | tf_op jit(solution)/shard_map/ppermute | solution.py:98
  172.1 10.0 %collective-permute-done.6 = bf16[128,512]{1,0:T(8,128)(2,1)S(1)} collective-permute-done((bf16[128,512]{1,0:T(8,128)(2,1)S(1)}, bf16[128,512]{1,0:T(8,128)(2,1)S(1)}, u32[]{:S(2)}, u32[]{:S(2)}) %collective-permute-start.6) | collective-permute-done | bytes 131104 | tf_op jit(solution)/shard_map/ppermute | solution.py:98
  182.2 10.0 %collective-permute-done.7 = bf16[128,512]{1,0:T(8,128)(2,1)S(1)} collective-permute-done((bf16[128,512]{1,0:T(8,128)(2,1)S(1)}, bf16[128,512]{1,0:T(8,128)(2,1)S(1)}, u32[]{:S(2)}, u32[]{:S(2)}) %collective-permute-start.7) | collective-permute-done | bytes 131104 | tf_op jit(solution)/shard_map/ppermute | solution.py:98
  192.2 10.0 %collective-permute-done.8 = bf16[128,512]{1,0:T(8,128)(2,1)S(1)} collective-permute-done((bf16[128,512]{1,0:T(8,128)(2,1)S(1)}, bf16[128,512]{1,0:T(8,128)(2,1)S(1)}, u32[]{:S(2)}, u32[]{:S(2)}) %collective-permute-start.8) | collective-permute-done | bytes 131104 | tf_op jit(solution)/shard_map/ppermute | solution.py:98
  202.2 10.0 %collective-permute-done.9 = bf16[128,512]{1,0:T(8,128)(2,1)S(1)} collective-permute-done((bf16[128,512]{1,0:T(8,128)(2,1)S(1)}, bf16[128,512]{1,0:T(8,128)(2,1)S(1)}, u32[]{:S(2)}, u32[]{:S(2)}) %collective-permute-start.9) | collective-permute-done | bytes 131104 | tf_op jit(solution)/shard_map/ppermute | solution.py:98
  212.2 10.0 %collective-permute-done.10 = bf16[128,512]{1,0:T(8,128)(2,1)S(1)} collective-permute-done((bf16[128,512]{1,0:T(8,128)(2,1)S(1)}, bf16[128,512]{1,0:T(8,128)(2,1)S(1)}, u32[]{:S(2)}, u32[]{:S(2)}) %collective-permute-start.10) | collective-permute-done | bytes 131104 | tf_op jit(solution)/shard_map/ppermute | solution.py:98
  222.3 10.0 %collective-permute-done.11 = bf16[128,512]{1,0:T(8,128)(2,1)S(1)} collective-permute-done((bf16[128,512]{1,0:T(8,128)(2,1)S(1)}, bf16[128,512]{1,0:T(8,128)(2,1)S(1)}, u32[]{:S(2)}, u32[]{:S(2)}) %collective-permute-start.11) | collective-permute-done | bytes 131104 | tf_op jit(solution)/shard_map/ppermute | solution.py:98
  232.3 10.0 %collective-permute-done.12 = bf16[128,512]{1,0:T(8,128)(2,1)S(1)} collective-permute-done((bf16[128,512]{1,0:T(8,128)(2,1)S(1)}, bf16[128,512]{1,0:T(8,128)(2,1)S(1)}, u32[]{:S(2)}, u32[]{:S(2)}) %collective-permute-start.12) | collective-permute-done | bytes 131104 | tf_op jit(solution)/shard_map/ppermute | solution.py:98
  242.3 9.3 %collective-permute-done.13 = bf16[128,512]{1,0:T(8,128)(2,1)S(1)} collective-permute-done((bf16[128,512]{1,0:T(8,128)(2,1)S(1)}, bf16[128,512]{1,0:T(8,128)(2,1)S(1)}, u32[]{:S(2)}, u32[]{:S(2)}) %collective-permute-start.13) | collective-permute-done | bytes 131104 | tf_op jit(solution)/shard_map/ppermute | solution.py:98
  252.3 6.4 %collective-permute-done.14 = bf16[128,512]{1,0:T(8,128)(2,1)S(1)} collective-permute-done((bf16[128,512]{1,0:T(8,128)(2,1)S(1)}, bf16[128,512]{1,0:T(8,128)(2,1)S(1)}, u32[]{:S(2)}, u32[]{:S(2)}) %collective-permute-start.14) | collective-permute-done | bytes 131104 | tf_op jit(solution)/shard_map/ppermute | solution.py:98
  259.3 1.5 constant_dynamic-slice_fusion.2
  260.9 2.9 copy.48
  263.8 8.2 %fusion.21 = f32[16,8,16,128]{3,1,2,0:T(8,128)S(1)} fusion(bf16[4096,2048]{1,0:T(8,128)(2,1)} %all-gather.13.cloned.1.call-done, f32[2048]{0:T(1024)S(1)} %convert_element_type.72, bf16[128,4096]{1,0:T(8,128)(2,1)S(1)} %copy-done, f32[4096]{0:T(1024)S(1)} %mul.214, f32[128]{0:T(128)S(1)} %add_rsqrt_fusion.1), kind=kOutput, calls=%fused_computation.38 | convolution fusion | flops 2149842944 | bytes 18899456 | tf_op jit(solution)/shard_map/dot_general | solution.py:58
  273.4 21.7 %all-gather.11.cloned.1.call-done = bf16[2048,512]{0,1:T(8,128)(2,1)} async-done(((bf16[128,512]{0,1:T(8,128)(2,1)}), bf16[2048,512]{0,1:T(8,128)(2,1)}) %all-gather.11.cloned.1.call-update) | async-done | bytes 2097168 | tf_op jit(solution)/shard_map/all_gather | solution.py:95
  295.1 1.1 broadcast_in_dim.105
  296.1 33.4 %while.20 = (s32[]{:T(128)}, f32[4,512]{1,0:T(4,128)S(1)}, f32[4,512]{1,0:T(4,128)S(1)}, f32[4,512,128]{2,1,0:T(8,128)}, s32[16]{0:T(128)S(1)}, /*index=5*/s32[]...) while((s32[]{:T(128)}, f32[4,512]{1,0:T(4,128)S(1)}, ...), condition=%wide.region_10.11_spmd.clone, body=%wide.region_3.10_spmd.clone.sunk | while | flops 551332864 | bytes 27935680 | solution.py:138
  298.2 6.3 %conditional.3 = ((f32[4,512]{1,0:T(4,128)S(1)}, f32[4,512]{1,0:T(4,128)S(1)}, f32[4,512,128]{2,1,0:T(8,128)})) conditional(s32[]{:T(128)} %convert_element_type.117, (f32[4,512]{1,0:T(4,128)S(1)}, f32[4,512]{1,0:T(4,128)S(1)}, f32[4,512,128]{2,1,0:T(8,128)}) %tuple.77, (s32[512]{0:T(512)S(1)}, s32[128]{0:T(128)S(1)}, s32[]{:T(128)}, ...), branch_computations={%region_6.6_spmd, %region_7.9_spmd} | conditional | flops 551292928 | bytes 27925118 | solution.py:136
  298.4 1.1 constant_dynamic-slice_fusion
  301.7 1.8 fusion.8
  306.5 6.3 %conditional.3 = ((f32[4,512]{1,0:T(4,128)S(1)}, f32[4,512]{1,0:T(4,128)S(1)}, f32[4,512,128]{2,1,0:T(8,128)})) conditional(s32[]{:T(128)} %convert_element_type.117, (f32[4,512]{1,0:T(4,128)S(1)}, f32[4,512]{1,0:T(4,128)S(1)}, f32[4,512,128]{2,1,0:T(8,128)}) %tuple.77, (s32[512]{0:T(512)S(1)}, s32[128]{0:T(128)S(1)}, s32[]{:T(128)}, ...), branch_computations={%region_6.6_spmd, %region_7.9_spmd} | conditional | flops 551292928 | bytes 27925118 | solution.py:136
  306.7 1.2 constant_dynamic-slice_fusion
  310.1 1.8 fusion.8
  314.9 6.3 %conditional.3 = ((f32[4,512]{1,0:T(4,128)S(1)}, f32[4,512]{1,0:T(4,128)S(1)}, f32[4,512,128]{2,1,0:T(8,128)})) conditional(s32[]{:T(128)} %convert_element_type.117, (f32[4,512]{1,0:T(4,128)S(1)}, f32[4,512]{1,0:T(4,128)S(1)}, f32[4,512,128]{2,1,0:T(8,128)}) %tuple.77, (s32[512]{0:T(512)S(1)}, s32[128]{0:T(128)S(1)}, s32[]{:T(128)}, ...), branch_computations={%region_6.6_spmd, %region_7.9_spmd} | conditional | flops 551292928 | bytes 27925118 | solution.py:136
  315.1 1.1 constant_dynamic-slice_fusion
  317.3 1.0 fusion.4
  318.4 1.8 fusion.8
  323.2 6.3 %conditional.3 = ((f32[4,512]{1,0:T(4,128)S(1)}, f32[4,512]{1,0:T(4,128)S(1)}, f32[4,512,128]{2,1,0:T(8,128)})) conditional(s32[]{:T(128)} %convert_element_type.117, (f32[4,512]{1,0:T(4,128)S(1)}, f32[4,512]{1,0:T(4,128)S(1)}, f32[4,512,128]{2,1,0:T(8,128)}) %tuple.77, (s32[512]{0:T(512)S(1)}, s32[128]{0:T(128)S(1)}, s32[]{:T(128)}, ...), branch_computations={%region_6.6_spmd, %region_7.9_spmd} | conditional | flops 551292928 | bytes 27925118 | solution.py:136
  323.5 1.1 constant_dynamic-slice_fusion
  326.7 1.8 fusion.8
  329.5 1.6 divide_convert_fusion
  331.4 94.7 %all-gather.15.cloned.1.call-done = bf16[2048,4096]{1,0:T(8,128)(2,1)} async-done(((bf16[2048,256]{1,0:T(8,128)(2,1)}), bf16[2048,4096]{1,0:T(8,128)(2,1)}) %all-gather.15.cloned.1.call-update) | async-done | bytes 16777232 | tf_op jit(solution)/shard_map/all_gather | solution.py:147
  426.1 9.2 %convolution_convert_fusion = bf16[128,4096]{1,0:T(8,128)(2,1)} fusion(bf16[128,2048]{0,1:T(8,128)(2,1)S(1)} %bitcast.52, bf16[2048,4096]{1,0:T(8,128)(2,1)} %all-gather.15.cloned.1.call-done), kind=kOutput, calls=%fused_computation.31 | convolution fusion | flops 2148007936 | bytes 18350080 | tf_op jit(solution)/shard_map/dot_general | solution.py:145
  435.4 18.7 %reduce-scatter.2.cloned.1.call-done = bf16[128,2048]{1,0:T(8,128)(2,1)} async-done(((bf16[128,4096]{1,0:T(8,128)(2,1)}), bf16[128,2048]{1,0:T(8,128)(2,1)}) %reduce-scatter.2.cloned.1.call-update) | async-done | bytes 524304 | tf_op jit(solution)/shard_map/reduce_scatter | solution.py:150
  454.1 1.3 multiply_reduce_fusion
  455.4 4.9 %psum.7 = f32[128]{0:T(128)S(1)} all-reduce(f32[128]{0:T(128)S(1)} %multiply_reduce_fusion), channel_id=1, replica_groups=mesh['seq'=16,'tp'=2] {'tp'}, use_global_device_ids=true, to_apply=%region_13.14 | all-reduce | flops 128 | bytes 1024 | tf_op jit(solution)/shard_map/psum | solution.py:155
  460.3 2.0 multiply_convert_fusion
  (149 shorter events, 22.8 us)
Async XLA Ops:
  7.2 26.4 %all-gather.7.cloned.1.call-start = ((), (), s32[]{:S(2)}) async-start(), calls=%async_computation.1 | async-start | bytes 1572864 | tf_op jit(solution)/shard_map/all_gather | solution.py:49
  7.9 102.8 %all-gather.9.cloned.1.call-start = ((), (), s32[]{:S(2)}) async-start(), calls=%async_computation.2 | async-start | bytes 8912896 | tf_op jit(solution)/shard_map/all_gather | solution.py:67
  9.9 254.0 %all-gather.13.cloned.1.call-start = ((), (), s32[]{:S(2)}) async-start(), calls=%async_computation.4 | async-start | bytes 17825792 | tf_op jit(solution)/shard_map/all_gather | solution.py:60
  10.6 284.5 %all-gather.11.cloned.1.call-start = ((), (), s32[]{:S(2)}) async-start(), calls=%async_computation.3 | async-start | bytes 2228224 | tf_op jit(solution)/shard_map/all_gather | solution.py:95
  35.1 216.5 %copy-start.5 = (bf16[2048]{0:T(1024)(128)(2,1)S(1)}, bf16[2048]{0:T(1024)(128)(2,1)}, u32[]{:S(2)}) copy-start(bf16[2048]{0:T(1024)(128)(2,1)} %param.17) | copy-start | bytes 12292
  117.1 309.0 %all-gather.15.cloned.1.call-start = ((), (), s32[]{:S(2)}) async-start(), calls=%async_computation.5 | async-start | bytes 17825792 | tf_op jit(solution)/shard_map/all_gather | solution.py:147
  117.7 336.4 %reduce-scatter.2.cloned.1.call-start = ((), (), s32[]{:S(2)}) async-start(), calls=%async_computation.6 | async-start | bytes 1572864 | tf_op jit(solution)/shard_map/reduce_scatter | solution.py:150
  117.8 7.2 %collective-permute-start = (bf16[128,512]{1,0:T(8,128)(2,1)S(1)}, bf16[128,512]{1,0:T(8,128)(2,1)S(1)}, u32[]{:S(2)}, u32[]{:S(2)}) collective-permute-start(bf16[128,512]{1,0:T(8,128)(2,1)S(1)} %fusion.25), channel_id=1, source_target_pairs={{0,2},{2,4},{4,6},{6,8},{8,10},{10,12},{12,14},{14,16},{16,18},{18... | collective-permute-start | bytes 393224 | tf_op jit(solution)/shard_map/ppermute | solution.py:98
  125.0 10.0 %collective-permute-start.1 = (bf16[128,512]{1,0:T(8,128)(2,1)S(1)}, bf16[128,512]{1,0:T(8,128)(2,1)S(1)}, u32[]{:S(2)}, u32[]{:S(2)}) collective-permute-start(bf16[128,512]{1,0:T(8,128)(2,1)S(1)} %collective-permute-done), channel_id=1, source_target_pairs={{0,2},{2,4},{4,6},{6,8},{8,10},{10,12},{12,14},{14,16},{16,18},{18... | collective-permute-start | bytes 393224 | tf_op jit(solution)/shard_map/ppermute | solution.py:98
  135.0 10.0 %collective-permute-start.2 = (bf16[128,512]{1,0:T(8,128)(2,1)S(1)}, bf16[128,512]{1,0:T(8,128)(2,1)S(1)}, u32[]{:S(2)}, u32[]{:S(2)}) collective-permute-start(bf16[128,512]{1,0:T(8,128)(2,1)S(1)} %collective-permute-done.1), channel_id=1, source_target_pairs={{0,2},{2,4},{4,6},{6,8},{8,10},{10,12},{12,14},{14,16},{16,18},{18... | collective-permute-start | bytes 393224 | tf_op jit(solution)/shard_map/ppermute | solution.py:98
  145.0 10.0 %collective-permute-start.3 = (bf16[128,512]{1,0:T(8,128)(2,1)S(1)}, bf16[128,512]{1,0:T(8,128)(2,1)S(1)}, u32[]{:S(2)}, u32[]{:S(2)}) collective-permute-start(bf16[128,512]{1,0:T(8,128)(2,1)S(1)} %collective-permute-done.2), channel_id=1, source_target_pairs={{0,2},{2,4},{4,6},{6,8},{8,10},{10,12},{12,14},{14,16},{16,18},{18... | collective-permute-start | bytes 393224 | tf_op jit(solution)/shard_map/ppermute | solution.py:98
  155.1 9.9 %collective-permute-start.4 = (bf16[128,512]{1,0:T(8,128)(2,1)S(1)}, bf16[128,512]{1,0:T(8,128)(2,1)S(1)}, u32[]{:S(2)}, u32[]{:S(2)}) collective-permute-start(bf16[128,512]{1,0:T(8,128)(2,1)S(1)} %collective-permute-done.3), channel_id=1, source_target_pairs={{0,2},{2,4},{4,6},{6,8},{8,10},{10,12},{12,14},{14,16},{16,18},{18... | collective-permute-start | bytes 393224 | tf_op jit(solution)/shard_map/ppermute | solution.py:98
  164.9 7.2 %collective-permute-start.5 = (bf16[128,512]{1,0:T(8,128)(2,1)S(1)}, bf16[128,512]{1,0:T(8,128)(2,1)S(1)}, u32[]{:S(2)}, u32[]{:S(2)}) collective-permute-start(bf16[128,512]{1,0:T(8,128)(2,1)S(1)} %collective-permute-done.4), channel_id=1, source_target_pairs={{0,2},{2,4},{4,6},{6,8},{8,10},{10,12},{12,14},{14,16},{16,18},{18... | collective-permute-start | bytes 393224 | tf_op jit(solution)/shard_map/ppermute | solution.py:98
  172.1 10.0 %collective-permute-start.6 = (bf16[128,512]{1,0:T(8,128)(2,1)S(1)}, bf16[128,512]{1,0:T(8,128)(2,1)S(1)}, u32[]{:S(2)}, u32[]{:S(2)}) collective-permute-start(bf16[128,512]{1,0:T(8,128)(2,1)S(1)} %collective-permute-done.5), channel_id=1, source_target_pairs={{0,2},{2,4},{4,6},{6,8},{8,10},{10,12},{12,14},{14,16},{16,18},{18... | collective-permute-start | bytes 393224 | tf_op jit(solution)/shard_map/ppermute | solution.py:98
  182.2 10.0 %collective-permute-start.7 = (bf16[128,512]{1,0:T(8,128)(2,1)S(1)}, bf16[128,512]{1,0:T(8,128)(2,1)S(1)}, u32[]{:S(2)}, u32[]{:S(2)}) collective-permute-start(bf16[128,512]{1,0:T(8,128)(2,1)S(1)} %collective-permute-done.6), channel_id=1, source_target_pairs={{0,2},{2,4},{4,6},{6,8},{8,10},{10,12},{12,14},{14,16},{16,18},{18... | collective-permute-start | bytes 393224 | tf_op jit(solution)/shard_map/ppermute | solution.py:98
  192.2 10.0 %collective-permute-start.8 = (bf16[128,512]{1,0:T(8,128)(2,1)S(1)}, bf16[128,512]{1,0:T(8,128)(2,1)S(1)}, u32[]{:S(2)}, u32[]{:S(2)}) collective-permute-start(bf16[128,512]{1,0:T(8,128)(2,1)S(1)} %collective-permute-done.7), channel_id=1, source_target_pairs={{0,2},{2,4},{4,6},{6,8},{8,10},{10,12},{12,14},{14,16},{16,18},{18... | collective-permute-start | bytes 393224 | tf_op jit(solution)/shard_map/ppermute | solution.py:98
  202.2 10.0 %collective-permute-start.9 = (bf16[128,512]{1,0:T(8,128)(2,1)S(1)}, bf16[128,512]{1,0:T(8,128)(2,1)S(1)}, u32[]{:S(2)}, u32[]{:S(2)}) collective-permute-start(bf16[128,512]{1,0:T(8,128)(2,1)S(1)} %collective-permute-done.8), channel_id=1, source_target_pairs={{0,2},{2,4},{4,6},{6,8},{8,10},{10,12},{12,14},{14,16},{16,18},{18... | collective-permute-start | bytes 393224 | tf_op jit(solution)/shard_map/ppermute | solution.py:98
  212.2 10.0 %collective-permute-start.10 = (bf16[128,512]{1,0:T(8,128)(2,1)S(1)}, bf16[128,512]{1,0:T(8,128)(2,1)S(1)}, u32[]{:S(2)}, u32[]{:S(2)}) collective-permute-start(bf16[128,512]{1,0:T(8,128)(2,1)S(1)} %collective-permute-done.9), channel_id=1, source_target_pairs={{0,2},{2,4},{4,6},{6,8},{8,10},{10,12},{12,14},{14,16},{16,18},{18... | collective-permute-start | bytes 393224 | tf_op jit(solution)/shard_map/ppermute | solution.py:98
  222.3 10.0 %collective-permute-start.11 = (bf16[128,512]{1,0:T(8,128)(2,1)S(1)}, bf16[128,512]{1,0:T(8,128)(2,1)S(1)}, u32[]{:S(2)}, u32[]{:S(2)}) collective-permute-start(bf16[128,512]{1,0:T(8,128)(2,1)S(1)} %collective-permute-done.10), channel_id=1, source_target_pairs={{0,2},{2,4},{4,6},{6,8},{8,10},{10,12},{12,14},{14,16},{16,18},{18... | collective-permute-start | bytes 393224 | tf_op jit(solution)/shard_map/ppermute | solution.py:98
  232.3 10.0 %collective-permute-start.12 = (bf16[128,512]{1,0:T(8,128)(2,1)S(1)}, bf16[128,512]{1,0:T(8,128)(2,1)S(1)}, u32[]{:S(2)}, u32[]{:S(2)}) collective-permute-start(bf16[128,512]{1,0:T(8,128)(2,1)S(1)} %collective-permute-done.11), channel_id=1, source_target_pairs={{0,2},{2,4},{4,6},{6,8},{8,10},{10,12},{12,14},{14,16},{16,18},{18... | collective-permute-start | bytes 393224 | tf_op jit(solution)/shard_map/ppermute | solution.py:98
  242.3 9.3 %collective-permute-start.13 = (bf16[128,512]{1,0:T(8,128)(2,1)S(1)}, bf16[128,512]{1,0:T(8,128)(2,1)S(1)}, u32[]{:S(2)}, u32[]{:S(2)}) collective-permute-start(bf16[128,512]{1,0:T(8,128)(2,1)S(1)} %collective-permute-done.12), channel_id=1, source_target_pairs={{0,2},{2,4},{4,6},{6,8},{8,10},{10,12},{12,14},{14,16},{16,18},{18... | collective-permute-start | bytes 393224 | tf_op jit(solution)/shard_map/ppermute | solution.py:98
  251.6 7.1 %collective-permute-start.14 = (bf16[128,512]{1,0:T(8,128)(2,1)S(1)}, bf16[128,512]{1,0:T(8,128)(2,1)S(1)}, u32[]{:S(2)}, u32[]{:S(2)}) collective-permute-start(bf16[128,512]{1,0:T(8,128)(2,1)S(1)} %collective-permute-done.13), channel_id=1, source_target_pairs={{0,2},{2,4},{4,6},{6,8},{8,10},{10,12},{12,14},{14,16},{16,18},{18... | collective-permute-start | bytes 393224 | tf_op jit(solution)/shard_map/ppermute | solution.py:98
  259.3 4.5 copy-start
  272.2 23.9 %copy-start.4 = (s32[16]{0:T(128)S(1)}, s32[16]{0:T(128)}, u32[]{:S(2)}) copy-start(s32[16]{0:T(128)} %param.14) | copy-start | bytes 196
  299.6 2.1 copy-start.2
  303.5 1.0 copy-start.3
  307.9 2.1 copy-start.2
  311.8 1.0 copy-start.3
  316.3 2.1 copy-start.2
  320.2 1.0 copy-start.3
  324.6 2.1 copy-start.2
  328.5 1.0 copy-start.3
  426.1 9.2 %copy-start.6 = (bf16[2048]{0:T(1024)(128)(2,1)S(1)}, bf16[2048]{0:T(1024)(128)(2,1)}, u32[]{:S(2)}) copy-start(bf16[2048]{0:T(1024)(128)(2,1)} %param.21) | copy-start | bytes 12292
  426.1 27.9 %copy-start.1 = (bf16[128,2048]{1,0:T(8,128)(2,1)S(1)}, bf16[128,2048]{1,0:T(8,128)(2,1)}, u32[]{:S(2)}) copy-start(bf16[128,2048]{1,0:T(8,128)(2,1)} %param.13) | copy-start | bytes 1572868
Sparse Core Ops, SparseCore 0:
  9.5 23.9 all-gather.6
  36.3 74.2 all-gather.8
  112.8 137.3 all-gather.12
  252.8 42.1 all-gather.10
  297.1 129.0 all-gather.14
  435.5 18.5 reduce-scatter.1
